TPU v7x, 32 devices: a whole 2x2x4 slice. The times are simulated.
32 devices in a mesh: grp: 8 (over z, x), ep: 4 (over y, core).
Axes of the slice: x: 2, y: 2, z: 4, core: 2. Of those that a mesh axis runs over, the one named last changes fastest.
Arguments:
- out_grad: bfloat16 [256, 4096], P('grp', 'ep'), may hold values from -6 to 6
- expert_ids: int32 [256, 8], P('grp'), may hold values from 0 to 15, as said below
- router_logits: float32 [256, 16], P('grp'), may hold values from -5 to 5
- router_weight: bfloat16 [16, 4096], P(None, 'ep'), may hold values from -0.09375 to 0.09375
- expert_weight: bfloat16 [16, 4096, 1024], P('grp', 'ep'), may hold values from -0.1875 to 0.1875
- hidden_saved: bfloat16 [8, 512, 1024], P('grp'), may hold values from -6 to 6
Outputs:
- weight_grad: bfloat16 [16, 4096, 1024], P('grp', 'ep')
- hidden_grad: bfloat16 [8, 512, 1024], P('grp', 'ep')
- input_grad: bfloat16 [256, 4096], P('grp', 'ep')
Inputs may be any that keep to these rules, and one draw needn't show every extreme that they name: `expert_ids`: each row names 8 different experts, lying in at most 4 of the 4 groups of 4 consecutive experts. In each aligned block of 32 rows no expert is named by more than 32 rows, and some expert is named by exactly 32.
All inputs are finite; a program needn't handle non-finite values.
Results may differ from a plain program's by a relative error of at most 0.02.
Values may be sent and summed in bfloat16 or wider, within the bound.
A program may use at most 64 MiB of HBM per device.

v0:
```python
import jax
import jax.numpy as jnp
from jax import lax
from jax.sharding import PartitionSpec as P

route_scale = 2.5


def body(out_grad, expert_ids, router_logits, router_weight, expert_weight, hidden_saved):
    group_rows, features = out_grad.shape
    top_count = expert_ids.shape[1]
    experts = router_logits.shape[1]
    group_count = lax.axis_size("grp")
    local_experts = expert_weight.shape[0]
    hidden_width = expert_weight.shape[2]
    slot_count = hidden_saved.shape[1]
    capacity = slot_count // (local_experts * group_count)
    expert_span = group_count * capacity
    pair_count = group_rows * top_count
    sig_values = jax.nn.sigmoid(router_logits)
    picked = expert_ids[:, :, None] == jnp.arange(experts, dtype=jnp.int32)[None, None, :]
    chosen = jnp.sum(jnp.where(picked, sig_values[:, None, :], 0.0), axis=2)
    route_probs = route_scale * chosen / jnp.sum(chosen, axis=1, keepdims=True)
    flat_ids = expert_ids.reshape(pair_count)
    onehot = picked.reshape(pair_count, experts).astype(jnp.int32)
    pair_ranks = jnp.sum((jnp.cumsum(onehot, axis=0) - 1) * onehot, axis=1)
    slot_place = (
        flat_ids % local_experts * group_count + flat_ids // local_experts
    ) * capacity + pair_ranks
    slot_match = slot_place[None, :] == jnp.arange(slot_count, dtype=jnp.int32)[:, None]
    token_pick = jnp.sum(
        slot_match.reshape(slot_count, group_rows, top_count).astype(jnp.float32), axis=2
    ).astype(jnp.bfloat16)
    send_rows = jnp.dot(token_pick, out_grad, preferred_element_type=jnp.float32).astype(
        jnp.bfloat16
    )
    send_prob = jnp.sum(
        jnp.where(slot_match, route_probs.reshape(1, pair_count), 0.0), axis=1
    ).astype(jnp.bfloat16)
    got_rows, got_prob = (
        lax.all_to_all(
            send_rows.reshape(local_experts, group_count, capacity, features),
            "grp",
            split_axis=1,
            concat_axis=1,
            tiled=True,
        ),
        lax.all_to_all(
            send_prob.reshape(local_experts, group_count, capacity),
            "grp",
            split_axis=1,
            concat_axis=1,
            tiled=True,
        ),
    )
    slot_grads = got_rows.reshape(local_experts, expert_span, features)
    prob_rows = got_prob.reshape(local_experts, expert_span).astype(jnp.float32)
    saved_rows = hidden_saved.reshape(local_experts, expert_span, hidden_width)
    scaled_rows = (prob_rows[:, :, None] * slot_grads.astype(jnp.float32)).astype(jnp.bfloat16)
    weight_grad = jnp.einsum(
        "lmd,lmf->ldf", scaled_rows, saved_rows, preferred_element_type=jnp.float32
    ).astype(jnp.bfloat16)
    owner_index = lax.axis_index("ep")
    share_rows = slot_count // lax.axis_size("ep")
    flat_prob = prob_rows.reshape(slot_count)
    flat_saved = hidden_saved.reshape(slot_count, hidden_width)
    partial_term = jnp.einsum(
        "lmd,ldf->lmf", slot_grads, expert_weight, preferred_element_type=jnp.float32
    ).reshape(slot_count, hidden_width)
    rounded_term = lax.optimization_barrier(partial_term.astype(jnp.bfloat16)).astype(jnp.float32)
    partial_score = jnp.sum(flat_saved.astype(jnp.float32) * rounded_term, axis=1)
    moved_scores = lax.all_to_all(
        partial_score.reshape(local_experts, group_count, capacity),
        "grp",
        split_axis=1,
        concat_axis=1,
        tiled=True,
    )
    returned = lax.psum(moved_scores, "ep")
    summed = lax.psum_scatter(
        partial_term.astype(jnp.bfloat16), "ep", scatter_dimension=0, tiled=True
    ).astype(jnp.float32)
    own_prob = lax.dynamic_slice_in_dim(flat_prob, owner_index * share_rows, share_rows, 0)
    hidden_grad = (own_prob[:, None] * summed).astype(jnp.bfloat16)[None]
    pair_score = jnp.sum(
        jnp.where(slot_match, returned.reshape(slot_count, 1), 0.0), axis=0
    ).reshape(group_rows, top_count)
    weighted_mean = jnp.sum(route_probs * pair_score, axis=1, keepdims=True) / route_scale
    logit_terms = route_probs * (1.0 - chosen) * (pair_score - weighted_mean)
    router_grad = jnp.sum(jnp.where(picked, logit_terms[:, :, None], 0.0), axis=1).astype(
        jnp.bfloat16
    )
    input_grad = jnp.dot(router_grad, router_weight, preferred_element_type=jnp.float32).astype(
        jnp.bfloat16
    )
    return (weight_grad, hidden_grad, input_grad)


def solution(mesh):
    in_specs = (
        P("grp", "ep"),
        P("grp", None),
        P("grp", None),
        P(None, "ep"),
        P("grp", "ep", None),
        P("grp", None, None),
    )
    out_specs = (P("grp", "ep", None), P("grp", "ep", None), P("grp", "ep"))
    return jax.shard_map(body, mesh=mesh, in_specs=in_specs, out_specs=out_specs, check_vma=False)
```

profile of v0, /device:TPU:0, one launch (start us, length us, event | category | flops | bytes accessed | tf_op | source)
XLA Modules:
  0.0 89.7 jit_solution(18396075402777026776)
XLA Ops:
  7.2 0.8 copy.70
  8.0 0.1 reshape.192
  8.2 0.6 reduce-window.6
  8.8 0.2 slice_reduce_fusion
  9.0 0.1 fusion.9
  9.2 0.2 convert_reduce_fusion
  9.4 0.4 convolution_convert_fusion.2
  9.9 1.1 %copy.80 = bf16[2,8,32,1024]{3,2,0,1:T(8,128)(2,1)} copy(bf16[2,8,32,1024]{3,2,1,0:T(8,128)(2,1)S(1)} %bitcast.33) | data formatting | bytes 2097152 | tf_op jit(solution)/shard_map/reshape | solution.py:42
  11.0 7.3 %all-to-all-start.1 = ((bf16[2,8,32,1024]{3,2,0,1:T(8,128)(2,1)}), bf16[2,8,32,1024]{3,2,0,1:T(8,128)(2,1)S(1)}, u32[]{:S(2)}, u32[]{:S(2)}) async-start(bf16[2,8,32,1024]{3,2,0,1:T(8,128)(2,1)} %copy.80), calls=%async_computation.1 | async-start | bytes 2097152 | tf_op jit(solution)/shard_map/all_to_all | solution.py:41
  18.4 25.7 %all-to-all-done.1 = bf16[2,8,32,1024]{3,2,0,1:T(8,128)(2,1)S(1)} async-done(((bf16[2,8,32,1024]{3,2,0,1:T(8,128)(2,1)}), bf16[2,8,32,1024]{3,2,0,1:T(8,128)(2,1)S(1)}, u32[]{:S(2)}, u32[]{:S(2)}) %all-to-all-start.1) | async-done | bytes 1048608 | tf_op jit(solution)/shard_map/all_to_all | solution.py:41
  44.1 4.5 %convolution_convert_fusion.1 = bf16[2,256,1024]{2,1,0:T(8,128)(2,1)} fusion(bf16[2,256,1024]{2,1,0:T(8,128)(2,1)S(1)} %bitcast.35, bf16[2,1024,1024]{2,1,0:T(8,128)(2,1)} %param.10), kind=kOutput, calls=%fused_computation.4 | convolution fusion | flops 1074266112 | bytes 6291456 | tf_op jit(solution)/shard_map/lmd,ldf->lmf/dot_general | solution.py:67
  48.7 1.6 %fusion = f32[512]{0:T(512)S(1)} fusion(bf16[512,1024]{1,0:T(8,128)(2,1)} %bitcast.32, bf16[1,512,1024]{2,1,0:T(8,128)(2,1)S(1)} %copy-done.1), kind=kLoop, calls=%fused_computation.2 | loop fusion | flops 2096640 | bytes 2099200 | tf_op jit(solution)/shard_map/reduce_sum | solution.py:71
  50.4 0.6 copy.83
  51.0 3.6 %all-to-all-start.2 = ((f32[2,8,32]{2,0,1:T(2,128)}), f32[2,8,32]{2,0,1:T(2,128)S(1)}, u32[]{:S(2)}, u32[]{:S(2)}) async-start(f32[2,8,32]{2,0,1:T(2,128)} %copy.83), calls=%async_computation.3 | async-start | bytes 16384 | tf_op jit(solution)/shard_map/all_to_all | solution.py:72
  54.7 0.1 div.50
  54.8 6.3 %all-to-all-done.2 = f32[2,8,32]{2,0,1:T(2,128)S(1)} async-done(((f32[2,8,32]{2,0,1:T(2,128)}), f32[2,8,32]{2,0,1:T(2,128)S(1)}, u32[]{:S(2)}, u32[]{:S(2)}) %all-to-all-start.2) | async-done | bytes 2080 | tf_op jit(solution)/shard_map/all_to_all | solution.py:72
  61.2 5.6 %psum.7 = f32[512]{0:T(512)S(1)} all-reduce(f32[512]{0:T(512)S(1)} %broadcast_in_dim.64), channel_id=1, replica_groups=mesh['grp'=8,'ep'=4] {'ep'}, use_global_device_ids=true, to_apply=%region_9.10 | all-reduce | flops 512 | bytes 4096 | tf_op jit(solution)/shard_map/psum | solution.py:79
  66.8 0.3 select_reduce_fusion
  67.2 0.6 copy.74
  67.8 3.3 %all-to-all-start = ((bf16[2,8,32]{2,0,1:T(2,128)(2,1)}), bf16[2,8,32]{2,0,1:T(2,128)(2,1)S(1)}, u32[]{:S(2)}, u32[]{:S(2)}) async-start(bf16[2,8,32]{2,0,1:T(2,128)(2,1)} %copy.74), calls=%async_computation | async-start | bytes 8192 | tf_op jit(solution)/shard_map/all_to_all | solution.py:48
  71.3 0.8 convolution_convert_fusion.3
  72.1 5.3 %all-to-all-done = bf16[2,8,32]{2,0,1:T(2,128)(2,1)S(1)} async-done(((bf16[2,8,32]{2,0,1:T(2,128)(2,1)}), bf16[2,8,32]{2,0,1:T(2,128)(2,1)S(1)}, u32[]{:S(2)}, u32[]{:S(2)}) %all-to-all-start) | async-done | bytes 1056 | tf_op jit(solution)/shard_map/all_to_all | solution.py:48
  77.7 3.4 %convolution_convert_fusion = bf16[2,1024,1024]{2,1,0:T(8,128)(2,1)} fusion(bf16[2,256,1024]{2,1,0:T(8,128)(2,1)S(1)} %bitcast.34, bf16[2,256,1024]{2,1,0:T(8,128)(2,1)S(1)} %bitcast.36, f32[2,256]{1,0:T(2,128)S(1)} %reshape.199), kind=kOutput, calls=%fused_computation | convolution fusion | flops 1077411840 | bytes 6293504 | tf_op jit(solution)/shard_map/lmd,lmf->ldf/dot_general | solution.py:60
  81.0 1.8 %fusion.2 = bf16[1,128,1024]{2,1,0:T(8,128)(2,1)} fusion(bf16[128,1024]{1,0:T(8,128)(2,1)} %reduce-scatter.2.cloned.1.call-done, f32[128]{0:T(128)S(1)} %dynamic_slice.3), kind=kLoop, calls=%fused_computation.14 | loop fusion | flops 393216 | bytes 524800 | tf_op jit(solution)/shard_map/broadcast_in_dim | solution.py:84
  (39 shorter events, 1.3 us)
Async XLA Ops:
  7.2 2.3 %copy-start = (bf16[32,1024]{1,0:T(8,128)(2,1)S(1)}, bf16[32,1024]{1,0:T(8,128)(2,1)}, u32[]{:S(2)}) copy-start(bf16[32,1024]{1,0:T(8,128)(2,1)} %param.6) | copy-start | bytes 196612
  9.9 8.4 %copy-start.4 = (f32[32,16]{0,1:T(8,128)S(1)}, f32[32,16]{0,1:T(8,128)}, u32[]{:S(2)}) copy-start(f32[32,16]{0,1:T(8,128)} %param.8) | copy-start | bytes 6148
  9.9 8.4 %copy-start.2 = (s32[32,8]{0,1:T(8,128)S(1)}, s32[32,8]{0,1:T(8,128)}, u32[]{:S(2)}) copy-start(s32[32,8]{0,1:T(8,128)} %param.7) | copy-start | bytes 3076
  11.0 33.0 %all-to-all-start.1 = ((bf16[2,8,32,1024]{3,2,0,1:T(8,128)(2,1)}), bf16[2,8,32,1024]{3,2,0,1:T(8,128)(2,1)S(1)}, u32[]{:S(2)}, u32[]{:S(2)}) async-start(bf16[2,8,32,1024]{3,2,0,1:T(8,128)(2,1)} %copy.80), calls=%async_computation.1 | async-start | bytes 2097152 | tf_op jit(solution)/shard_map/all_to_all | solution.py:41
  18.3 62.8 %reduce-scatter.2.cloned.1.call-start = ((), (), s32[]{:S(2)}) async-start(), calls=%async_computation.4 | async-start | bytes 1310720 | tf_op jit(solution)/shard_map/reduce_scatter | solution.py:80
  44.1 4.6 %copy-start.1 = (bf16[1,512,1024]{2,1,0:T(8,128)(2,1)S(1)}, bf16[1,512,1024]{2,1,0:T(8,128)(2,1)}, u32[]{:S(2)}) copy-start(bf16[1,512,1024]{2,1,0:T(8,128)(2,1)} %param.11) | copy-start | bytes 3145732
  48.7 22.6 %copy-start.3 = (bf16[16,1024]{1,0:T(8,128)(2,1)S(1)}, bf16[16,1024]{1,0:T(8,128)(2,1)}, u32[]{:S(2)}) copy-start(bf16[16,1024]{1,0:T(8,128)(2,1)} %param.9) | copy-start | bytes 98308
  51.0 10.1 %all-to-all-start.2 = ((f32[2,8,32]{2,0,1:T(2,128)}), f32[2,8,32]{2,0,1:T(2,128)S(1)}, u32[]{:S(2)}, u32[]{:S(2)}) async-start(f32[2,8,32]{2,0,1:T(2,128)} %copy.83), calls=%async_computation.3 | async-start | bytes 16384 | tf_op jit(solution)/shard_map/all_to_all | solution.py:72
  67.8 9.7 %all-to-all-start = ((bf16[2,8,32]{2,0,1:T(2,128)(2,1)}), bf16[2,8,32]{2,0,1:T(2,128)(2,1)S(1)}, u32[]{:S(2)}, u32[]{:S(2)}) async-start(bf16[2,8,32]{2,0,1:T(2,128)(2,1)} %copy.74), calls=%async_computation | async-start | bytes 8192 | tf_op jit(solution)/shard_map/all_to_all | solution.py:48
Sparse Core Ops, SparseCore 0:
  48.8 23.8 reduce-scatter.1
where the time goes:
time: 90 us; the launch traced here: 89.7 us
  waiting for transfers between devices  37.3 us (41%)
  starting transfers between devices  14.2 us (16%)
  between operations  14.2 us (16%)
  matrix products  9.16 us (10%)
  blocking collectives  5.63 us (6%)
  other arithmetic  4.71 us (5%)
  local copies, waits for them, and re-layouts  4.43 us (5%)
    all_to_all x1, waiting for transfers between devices, body(): lax.all_to_all(send_rows.reshape(local_experts, group_count, capacity, fe...  25.7 us
    all_to_all x1, starting transfers between devices, body(): lax.all_to_all(send_rows.reshape(local_experts, group_count, capacity, fe...  7.28 us
    all_to_all x1, waiting for transfers between devices, body(): lax.all_to_all(partial_score.reshape(local_experts, group_count, capacity...  6.34 us
    psum x1, blocking collectives, body(): returned = lax.psum(moved_scores, 'ep')  5.63 us
    all_to_all x1, waiting for transfers between devices, body(): lax.all_to_all(send_prob.reshape(local_experts, group_count, capacity), '...  5.3 us
    dot_general x1, matrix products, body(): jnp.einsum('lmd,ldf->lmf', slot_grads, expert_weight, preferred_element_t...  4.52 us
    all_to_all x1, starting transfers between devices, body(): lax.all_to_all(partial_score.reshape(local_experts, group_count, capacity...  3.59 us
    dot_general x1, matrix products, body(): jnp.einsum('lmd,lmf->ldf', scaled_rows, saved_rows, preferred_element_typ...  3.38 us
  transfers between devices with their start and end apart: 4, of which 3 were waited for; matrix products, arithmetic and copies ran while one was open for 9% of the time, Pallas kernels for 0%

commit v1 on v0

--- a/solution.py
+++ b/solution.py
@@ -1,6 +1,8 @@
 import jax
 import jax.numpy as jnp
 from jax import lax
+from jax.experimental import pallas as pl
+from jax.experimental.pallas import tpu as pltpu
 from jax.sharding import PartitionSpec as P
 
 route_scale = 2.5
@@ -96,6 +98,353 @@
     return (weight_grad, hidden_grad, input_grad)
 
 
+MESH = pl.DeviceIdType.MESH
+
+
+def fused_kernel(
+    ids_ref, logits_ref, grad_ref, rw_ref, w_hbm, saved_hbm,
+    scaled_ref, hidden_ref, input_ref,
+    w_ref, saved_ref, rows_all, probs_all, probs_own, slot_ref, slot_rows, prob_col, part,
+    recv_a, send_b, recv_b, score_own, score_recv, score_rows,
+    w_sem, saved_sem, rows_send, rows_recv, probs_send, probs_recv,
+    a_send, a_recv, b_send, b_recv, sc_send, sc_recv,
+):
+    groups = lax.axis_size("grp")
+    parts = lax.axis_size("ep")
+    chips = parts // 2
+    g = lax.axis_index("grp")
+    k = lax.axis_index("ep")
+    chip, core = k // 2, k % 2
+    rows, features = grad_ref.shape
+    experts = logits_ref.shape[0]
+    top = ids_ref.shape[0]
+    local, span, width = part.shape
+    half_groups = groups // 2
+    half_tokens = half_groups * rows
+    tokens = groups * rows
+    share = span // 2
+    capacity = span // groups
+    f32, bf16 = jnp.float32, jnp.bfloat16
+
+    barrier = pltpu.get_barrier_semaphore()
+    for dg in range(groups):
+        for dk in range(parts):
+            if dg or dk:
+                pl.semaphore_signal(
+                    barrier, inc=1,
+                    device_id=(lax.rem(g + dg, groups), lax.rem(k + dk, parts)),
+                    device_id_type=MESH,
+                )
+    w_copies = [
+        pltpu.make_async_copy(w_hbm.at[i], w_ref.at[i], w_sem.at[i]) for i in range(local)
+    ]
+    for copy in w_copies:
+        copy.start()
+    saved_copy = pltpu.make_async_copy(saved_hbm, saved_ref, saved_sem)
+    saved_copy.start()
+
+    sig = 1.0 / (1.0 + jnp.exp(-logits_ref[...]))
+    ids = ids_ref[...]
+    expert_iota = lax.broadcasted_iota(jnp.int32, (experts, rows), 0)
+    named = ids[0:1, :] == expert_iota
+    for i in range(1, top):
+        named = named | (ids[i : i + 1, :] == expert_iota)
+    probs = route_scale * sig / jnp.sum(jnp.where(named, sig, 0.0), axis=0, keepdims=True)
+    probs = jnp.where(named, probs, 0.0)
+    lane_off = lax.rem(g, half_groups) * rows
+    place = (
+        lax.broadcasted_iota(jnp.int32, (rows, half_tokens), 1)
+        == lax.broadcasted_iota(jnp.int32, (rows, half_tokens), 0) + lane_off
+    )
+    placed = jnp.dot(
+        probs.astype(bf16), place.astype(f32).astype(bf16), preferred_element_type=f32
+    ).astype(bf16)
+    probs_own[...] = placed
+    probs_all[g] = placed
+    rows_all[pl.ds(pl.multiple_of(g * rows, rows), rows), :] = grad_ref[...]
+
+    pl.semaphore_wait(barrier, groups * parts - 1)
+
+    parity, pos = lax.rem(g, 2), g // 2
+    mate = g + 1 - 2 * parity
+
+    def block(b):
+        return rows_all.at[pl.ds(pl.multiple_of(b * rows, rows), rows), :]
+
+    def rows_copy(src, b, to, sem):
+        return pltpu.make_async_remote_copy(
+            src_ref=src, dst_ref=block(b), send_sem=rows_send.at[sem], recv_sem=rows_recv.at[b],
+            device_id=(to, k), device_id_type=MESH,
+        )
+
+    sends = []
+    peers = [lax.rem(pos + j, half_groups) * 2 + parity for j in range(1, half_groups)]
+    for j in range(1, groups):
+        to = lax.rem(g + j, groups)
+        copy = pltpu.make_async_remote_copy(
+            src_ref=probs_own, dst_ref=probs_all.at[g],
+            send_sem=probs_send.at[j - 1], recv_sem=probs_recv.at[g],
+            device_id=(to, k), device_id_type=MESH,
+        )
+        copy.start()
+        sends.append(copy)
+    for n, to in enumerate([*peers, mate]):
+        copy = rows_copy(grad_ref, g, to, n)
+        copy.start()
+        sends.append(copy)
+    for n, peer in enumerate(peers):
+        rows_copy(block(peer), peer, g, 0).wait_recv()
+        copy = rows_copy(block(peer), peer, mate, half_groups + n)
+        copy.start()
+        sends.append(copy)
+
+    for j in range(1, groups):
+        b = lax.rem(g + j, groups)
+        pltpu.make_async_remote_copy(
+            src_ref=probs_own, dst_ref=probs_all.at[b],
+            send_sem=probs_send.at[0], recv_sem=probs_recv.at[b],
+            device_id=(g, k), device_id_type=MESH,
+        ).wait_recv()
+    pick = (
+        lax.broadcasted_iota(jnp.int32, (8, experts), 1)
+        == lax.broadcasted_iota(jnp.int32, (8, experts), 0) + g * local
+    ) & (lax.broadcasted_iota(jnp.int32, (8, experts), 0) < local)
+    pick = pick.astype(f32).astype(bf16)
+    halves = []
+    for h in range(2):
+        total = probs_all[h * half_groups].astype(f32)
+        for b in range(1, half_groups):
+            total = total + probs_all[h * half_groups + b].astype(f32)
+        halves.append(jnp.dot(pick, total.astype(bf16), preferred_element_type=f32))
+    lane = lax.broadcasted_iota(jnp.int32, (half_tokens, half_tokens), 1)
+    before = lax.broadcasted_iota(jnp.int32, (half_tokens, half_tokens), 0)
+    earlier = (before < lane) & (before // rows == lane // rows)
+    earlier = earlier.astype(f32).astype(bf16)
+    half_block = lax.broadcasted_iota(jnp.int32, (8, half_tokens), 1) // rows
+    for h in range(2):
+        used = halves[h] > 0.0
+        rank = jnp.dot(used.astype(f32).astype(bf16), earlier, preferred_element_type=f32)
+        slot = (half_block + h * half_groups) * capacity + rank.astype(jnp.int32)
+        slot_ref[h] = jnp.where(used, slot, -1)
+    prob_tokens = jnp.concatenate(halves, axis=1)
+
+    def slot_row(l, h):
+        table = slot_ref[h]
+        mask = lax.broadcasted_iota(jnp.int32, table.shape, 0) == l
+        return jnp.sum(jnp.where(mask, table, 0), axis=0, keepdims=True)
+
+    for l in range(local):
+        row = jnp.concatenate([slot_row(l, 0), slot_row(l, 1)], axis=1)
+        match = lax.broadcasted_iota(jnp.int32, (span, tokens), 0) == row
+        prob_col[l] = jnp.sum(
+            jnp.where(match, prob_tokens[l : l + 1, :], 0.0), axis=1, keepdims=True
+        )
+
+    rows_copy(grad_ref, mate, g, 0).wait_recv()
+    for n, peer in enumerate(peers):
+        b = peer + 1 - 2 * parity
+        rows_copy(grad_ref, b, g, 0).wait_recv()
+    for copy in w_copies:
+        copy.wait()
+
+    order = [lax.rem(chip + 1 + i, chips) for i in range(chips)]
+
+    def a_copy(l, half, to):
+        return pltpu.make_async_remote_copy(
+            src_ref=part.at[l, pl.ds(pl.multiple_of(half * share, share), share), :],
+            dst_ref=recv_a.at[l], send_sem=a_send.at[l], recv_sem=a_recv.at[l],
+            device_id=(g, to), device_id_type=MESH,
+        )
+
+    def b_copy(l):
+        return pltpu.make_async_remote_copy(
+            src_ref=send_b.at[l], dst_ref=recv_b.at[chip],
+            send_sem=b_send.at[l], recv_sem=b_recv.at[chip],
+            device_id=(g, l * 2 + core), device_id_type=MESH,
+        )
+
+    partner = k + 1 - 2 * core
+    step = min(width, 256)
+    for l in order:
+        row = jnp.concatenate([slot_row(l, 0), slot_row(l, 1)], axis=1)
+        match = lax.broadcasted_iota(jnp.int32, (span, tokens), 0) == row
+        slot_rows[l] = jnp.dot(
+            match.astype(f32).astype(bf16), rows_all[...], preferred_element_type=f32
+        ).astype(bf16)
+        for n in range(0, width, step):
+            part[l, :, n : n + step] = jnp.dot(
+                slot_rows[l], w_ref[l, :, n : n + step], preferred_element_type=f32
+            ).astype(bf16)
+        copy = a_copy(l, 1 - core, partner)
+        copy.start()
+        sends.append(copy)
+
+    saved_copy.wait()
+    kept = pl.ds(pl.multiple_of(core * share, share), share)
+    for i, l in enumerate(order):
+        a_copy(l, 1 - core, partner).wait_recv()
+        both = part[l, kept, :].astype(f32) + recv_a[l].astype(f32)
+        send_b[l] = both.astype(bf16)
+        if i < chips - 1:
+            copy = b_copy(l)
+            copy.start()
+            sends.append(copy)
+        start = pl.multiple_of(l * span + core * share, share)
+        score = jnp.sum(
+            saved_ref[pl.ds(start, share), :].astype(f32) * both, axis=1, keepdims=True
+        )
+        match = (
+            lax.broadcasted_iota(jnp.int32, (share, half_tokens), 0) + core * share
+            == slot_row(l, core)
+        )
+        score_own[pl.ds(l, 1), :] = jnp.sum(jnp.where(match, score, 0.0), axis=0, keepdims=True)
+
+    def score_copy(b, to, sem, y, o):
+        return pltpu.make_async_remote_copy(
+            src_ref=score_own, dst_ref=score_recv.at[y, o],
+            send_sem=sc_send.at[sem], recv_sem=sc_recv.at[y * groups + o],
+            device_id=(b, to), device_id_type=MESH,
+        )
+
+    for j in range(half_groups):
+        b = core * half_groups + j
+        for dk in range(parts):
+            copy = score_copy(b, lax.rem(k + dk, parts), j * parts + dk, chip, g)
+            if dk:
+                copy.start()
+            else:
+                pl.when(b != g)(copy.start)
+
+    my_half = g // half_groups
+
+    @pl.when(my_half == core)
+    def _():
+        score_recv[chip, g] = score_own[...]
+
+    for l in range(local):
+        scaled_ref[l] = (prob_col[l] * slot_rows[l].astype(f32)).astype(bf16)
+
+    for i in range(chips - 1):
+        source = order[i]
+        pltpu.make_async_remote_copy(
+            src_ref=send_b.at[0], dst_ref=recv_b.at[source],
+            send_sem=b_send.at[0], recv_sem=b_recv.at[source],
+            device_id=(g, k), device_id_type=MESH,
+        ).wait_recv()
+    total = send_b[chip].astype(f32)
+    for i in range(chips - 1):
+        total = total + recv_b[order[i]].astype(f32)
+    hidden_ref[...] = (prob_col[chip, kept, :] * total).astype(bf16)
+
+    for y in range(chips):
+        for o in range(groups):
+            wait = score_copy(g, k, 0, y, o).wait_recv
+            pl.when((o != g) | (y != chip) | (my_half != core))(wait)
+    for o in range(groups):
+        value = score_recv[0, o]
+        for y in range(1, chips):
+            value = value + score_recv[y, o]
+        score_rows[o * local : (o + 1) * local, :] = value
+    take = (
+        lax.broadcasted_iota(jnp.int32, (half_tokens, rows), 0)
+        == lax.broadcasted_iota(jnp.int32, (half_tokens, rows), 1) + lane_off
+    )
+    pair = jnp.dot(
+        score_rows[...], take.astype(f32), preferred_element_type=f32,
+        precision=lax.Precision.HIGHEST,
+    )
+    mean = jnp.sum(probs * pair, axis=0, keepdims=True) / route_scale
+    terms = jnp.where(named, probs * (1.0 - sig) * (pair - mean), 0.0).astype(bf16)
+    eye = (
+        lax.broadcasted_iota(jnp.int32, (rows, rows), 0)
+        == lax.broadcasted_iota(jnp.int32, (rows, rows), 1)
+    )
+    turned = lax.dot_general(
+        eye.astype(f32).astype(bf16), terms, (((1,), (1,)), ((), ())), preferred_element_type=f32
+    ).astype(bf16)
+    input_ref[...] = jnp.dot(turned, rw_ref[...], preferred_element_type=f32).astype(bf16)
+
+    for copy in sends:
+        copy.wait_send()
+    for j in range(half_groups):
+        b = core * half_groups + j
+        for dk in range(parts):
+            wait = score_copy(b, lax.rem(k + dk, parts), j * parts + dk, chip, g).wait_send
+            if dk:
+                wait()
+            else:
+                pl.when(b != g)(wait)
+
+
+def fused(out_grad, expert_ids, router_logits, router_weight, expert_weight, hidden_saved):
+    groups, parts = lax.axis_size("grp"), lax.axis_size("ep")
+    rows, features = out_grad.shape
+    experts = router_logits.shape[1]
+    local, _, width = expert_weight.shape
+    slots = hidden_saved.shape[1]
+    span = slots // local
+    half_tokens = groups // 2 * rows
+    share = span // 2
+    chips = parts // 2
+    f32, bf16 = jnp.float32, jnp.bfloat16
+    vmem = pl.BlockSpec(memory_space=pltpu.VMEM)
+    anyspace = pl.BlockSpec(memory_space=pl.ANY)
+    dma = pltpu.SemaphoreType.DMA
+    scaled, hidden, input_grad = pl.pallas_call(
+        fused_kernel,
+        out_shape=(
+            jax.ShapeDtypeStruct((local, span, features), bf16),
+            jax.ShapeDtypeStruct((share, width), bf16),
+            jax.ShapeDtypeStruct((rows, features), bf16),
+        ),
+        in_specs=[vmem, vmem, vmem, vmem, anyspace, anyspace],
+        out_specs=(vmem, vmem, vmem),
+        scratch_shapes=[
+            pltpu.VMEM((local, features, width), bf16),
+            pltpu.VMEM((slots, width), bf16),
+            pltpu.VMEM((groups * rows, features), bf16),
+            pltpu.VMEM((groups, experts, half_tokens), bf16),
+            pltpu.VMEM((experts, half_tokens), bf16),
+            pltpu.VMEM((2, 8, half_tokens), jnp.int32),
+            pltpu.VMEM((local, span, features), bf16),
+            pltpu.VMEM((local, span, 1), f32),
+            pltpu.VMEM((local, span, width), bf16),
+            pltpu.VMEM((local, share, width), bf16),
+            pltpu.VMEM((local, share, width), bf16),
+            pltpu.VMEM((chips, share, width), bf16),
+            pltpu.VMEM((local, half_tokens), f32),
+            pltpu.VMEM((chips, groups, local, half_tokens), f32),
+            pltpu.VMEM((experts, half_tokens), f32),
+            dma((local,)), dma, dma((groups - 1,)), dma((groups,)),
+            dma((groups - 1,)), dma((groups,)),
+            dma((local,)), dma((local,)), dma((local,)), dma((chips,)),
+            dma((groups // 2 * parts,)), dma((chips * groups,)),
+        ],
+        compiler_params=pltpu.CompilerParams(
+            collective_id=0, has_side_effects=True, vmem_limit_bytes=40 * 1024 * 1024
+        ),
+    )(
+        expert_ids.T, router_logits.T, out_grad, router_weight, expert_weight,
+        hidden_saved.reshape(slots, width),
+    )
+    saved_rows = hidden_saved.reshape(local, span, width)
+    weight_grad = jnp.einsum(
+        "lmd,lmf->ldf", scaled, saved_rows, preferred_element_type=f32
+    ).astype(bf16)
+    return weight_grad, hidden[None], input_grad
+
+
+def choose(*args):
+    out_grad, _, _, _, expert_weight, hidden_saved = args
+    groups, parts = lax.axis_size("grp"), lax.axis_size("ep")
+    rows, local = out_grad.shape[0], expert_weight.shape[0]
+    slots_for_one = hidden_saved.shape[1] // groups
+    lanes = groups // 2 * rows
+    if parts == 2 * local and groups % 2 == 0 and rows <= slots_for_one and lanes % 128 == 0:
+        return fused(*args)
+    return body(*args)
+
+
 def solution(mesh):
     in_specs = (
         P("grp", "ep"),
@@ -106,4 +455,4 @@
         P("grp", None, None),
     )
     out_specs = (P("grp", "ep", None), P("grp", "ep", None), P("grp", "ep"))
-    return jax.shard_map(body, mesh=mesh, in_specs=in_specs, out_specs=out_specs, check_vma=False)
+    return jax.shard_map(choose, mesh=mesh, in_specs=in_specs, out_specs=out_specs, check_vma=False)

time: 90 us -> 41.2 us (0.46)
  waiting for transfers between devices: 37.3 us -> 0 us
  Pallas kernels: 0 us -> 28.8 us
  starting transfers between devices: 14.2 us -> 0 us
  between operations: 14.2 us -> 0.65 us
  matrix products: 9.16 us -> 3.32 us
  blocking collectives: 5.63 us -> 0 us
  other arithmetic: 4.71 us -> 0 us
  local copies, waits for them, and re-layouts: 4.43 us -> 7.72 us
    all_to_all x3 -> x0, waiting for transfers between devices: 37.3 us -> none  [the longest x1 25.7 us: body(): lax.all_to_all(send_rows.reshape(local_experts, group_count, capacity, fe...]
    pallas_call x0 -> x1, Pallas kernels: none -> 28.8 us  [fused(): pl.pallas_call(fused_kernel, out_shape=(jax.ShapeDtypeStruct((local, span...]
    all_to_all x3 -> x0, starting transfers between devices: 14.2 us -> none  [the longest x1 7.28 us: body(): lax.all_to_all(send_rows.reshape(local_experts, group_count, capacity, fe...]
    unnamed x11 -> x14, local copies, waits for them, and re-layouts: 0.83 us -> 7.72 us
    dot_general x4 -> x1, matrix products: 9.16 us -> 3.32 us  [fused(): jnp.einsum('lmd,lmf->ldf', scaled, saved_rows, preferred_element_type=f32)]
    psum x1 -> x0, blocking collectives: 5.63 us -> none  [body(): returned = lax.psum(moved_scores, 'ep')]
    reduce_sum x7 -> x0, other arithmetic: 2.23 us -> none  [the longest x1 1.57 us: body(): jnp.sum(flat_saved.astype(jnp.float32) * rounded_term, axis=1)]
    reshape x6 -> x0, local copies, waits for them, and re-layouts: 1.99 us -> none  [the longest x1 1.06 us: body(): send_rows.reshape(local_experts, group_count, capacity, features)]
  transfers between devices with their start and end apart: 4 -> 0, of which waited for: 3 -> 0; matrix products, arithmetic and copies ran while one was open for 9% -> 0% of each run, Pallas kernels for 0% -> 0%
where the time goes in v1:
time: 41.2 us; the launch traced here: 40.4 us
  Pallas kernels  28.8 us (70%)
  local copies, waits for them, and re-layouts  7.72 us (19%)
  matrix products  3.32 us (8%)
  between operations  0.65 us (2%)
    pallas_call x1, Pallas kernels, fused(): pl.pallas_call(fused_kernel, out_shape=(jax.ShapeDtypeStruct((local, span...  28.8 us
    unnamed x14, local copies, waits for them, and re-layouts  7.72 us
    dot_general x1, matrix products, fused(): jnp.einsum('lmd,lmf->ldf', scaled, saved_rows, preferred_element_type=f32)  3.32 us

profile of v1, /device:TPU:0, one launch (start us, length us, event | category | flops | bytes accessed | tf_op | source)
XLA Modules:
  0.0 40.4 jit_solution(17395211627296477204)
XLA Ops:
  0.6 0.0 copy-start
  0.6 2.2 %copy-done = bf16[2,1024,1024]{2,1,0:T(8,128)(2,1)S(1)} copy-done((bf16[2,1024,1024]{2,1,0:T(8,128)(2,1)S(1)}, bf16[2,1024,1024]{2,1,0:T(8,128)(2,1)}, u32[]{:S(2)}) %copy-start) | copy-done | bytes 4194328
  2.8 0.0 copy-start.1
  2.8 1.2 %copy-done.1 = bf16[1,512,1024]{2,1,0:T(8,128)(2,1)S(1)} copy-done((bf16[1,512,1024]{2,1,0:T(8,128)(2,1)S(1)}, bf16[1,512,1024]{2,1,0:T(8,128)(2,1)}, u32[]{:S(2)}) %copy-start.1) | copy-done | bytes 1048600
  4.0 0.0 copy-start.2
  4.0 0.8 %copy-done.2 = bf16[32,1024]{1,0:T(8,128)(2,1)S(1)} copy-done((bf16[32,1024]{1,0:T(8,128)(2,1)S(1)}, bf16[32,1024]{1,0:T(8,128)(2,1)}, u32[]{:S(2)}) %copy-start.2) | copy-done | bytes 65560
  4.9 0.0 copy-start.3
  4.9 0.8 %copy-done.3 = bf16[16,1024]{1,0:T(8,128)(2,1)S(1)} copy-done((bf16[16,1024]{1,0:T(8,128)(2,1)S(1)}, bf16[16,1024]{1,0:T(8,128)(2,1)}, u32[]{:S(2)}) %copy-start.3) | copy-done | bytes 32792
  5.6 0.0 copy-start.4
  5.6 0.7 %copy-done.4 = f32[32,16]{0,1:T(8,128)S(1)} copy-done((f32[32,16]{0,1:T(8,128)S(1)}, f32[32,16]{0,1:T(8,128)}, u32[]{:S(2)}) %copy-start.4) | copy-done | bytes 2072
  6.3 0.0 copy-start.5
  6.3 0.7 %copy-done.5 = s32[32,8]{0,1:T(8,128)S(1)} copy-done((s32[32,8]{0,1:T(8,128)S(1)}, s32[32,8]{0,1:T(8,128)}, u32[]{:S(2)}) %copy-start.5) | copy-done | bytes 1048
  7.0 28.8 %shard_map.85 = (bf16[2,256,1024]{2,1,0:T(8,128)(2,1)S(1)}, bf16[128,1024]{1,0:T(8,128)(2,1)S(1)}, bf16[32,1024]{1,0:T(8,128)(2,1)S(1)}) custom-call(s32[8,32]{1,0:T(8,128)S(1)} %bitcast.11, f32[16,32]{1,0:T(8,128)S(1)} %bitcast.10, bf16[32,1024]{1,0:T(8,128)(2,1)S(1)} %copy-done.2, bf16[16,1024]{1,0:T(8,128)(2,1)S(1)} %copy-done.3, ...), custom_call_target="tpu_custom_call" | custom-call | tf_op jit(solution)/shard_map/pallas_call | solution.py:393
  35.8 3.3 %convolution_convert_fusion = bf16[2,1024,1024]{2,1,0:T(8,128)(2,1)} fusion(bf16[2,256,1024]{2,1,0:T(8,128)(2,1)S(1)} %get-tuple-element.6, bf16[2,256,1024]{2,1,0:T(8,128)(2,1)S(1)} %bitcast.8), kind=kOutput, calls=%fused_computation | convolution fusion | flops 1075838976 | bytes 6291456 | tf_op jit(solution)/shard_map/lmd,lmf->ldf/dot_general | solution.py:431
  39.1 0.7 %copy.13 = bf16[1,128,1024]{2,1,0:T(8,128)(2,1)} copy(bf16[1,128,1024]{2,1,0:T(8,128)(2,1)S(1)} %bitcast.9) | data formatting | bytes 524288
  39.8 0.6 %copy.14 = bf16[32,1024]{1,0:T(8,128)(2,1)} copy(bf16[32,1024]{1,0:T(8,128)(2,1)S(1)} %get-tuple-element.14) | data formatting | bytes 131072
Async XLA Ops:
  0.6 2.2 %copy-start = (bf16[2,1024,1024]{2,1,0:T(8,128)(2,1)S(1)}, bf16[2,1024,1024]{2,1,0:T(8,128)(2,1)}, u32[]{:S(2)}) copy-start(bf16[2,1024,1024]{2,1,0:T(8,128)(2,1)} %w_hbm.1) | copy-start | bytes 12582916
  2.8 1.2 %copy-start.1 = (bf16[1,512,1024]{2,1,0:T(8,128)(2,1)S(1)}, bf16[1,512,1024]{2,1,0:T(8,128)(2,1)}, u32[]{:S(2)}) copy-start(bf16[1,512,1024]{2,1,0:T(8,128)(2,1)} %param.11) | copy-start | bytes 3145732
  4.0 0.8 %copy-start.2 = (bf16[32,1024]{1,0:T(8,128)(2,1)S(1)}, bf16[32,1024]{1,0:T(8,128)(2,1)}, u32[]{:S(2)}) copy-start(bf16[32,1024]{1,0:T(8,128)(2,1)} %grad_ref.1) | copy-start | bytes 196612
  4.9 0.8 %copy-start.3 = (bf16[16,1024]{1,0:T(8,128)(2,1)S(1)}, bf16[16,1024]{1,0:T(8,128)(2,1)}, u32[]{:S(2)}) copy-start(bf16[16,1024]{1,0:T(8,128)(2,1)} %rw_ref.1) | copy-start | bytes 98308
  5.6 0.7 %copy-start.4 = (f32[32,16]{0,1:T(8,128)S(1)}, f32[32,16]{0,1:T(8,128)}, u32[]{:S(2)}) copy-start(f32[32,16]{0,1:T(8,128)} %param.8) | copy-start | bytes 6148
  6.3 0.7 %copy-start.5 = (s32[32,8]{0,1:T(8,128)S(1)}, s32[32,8]{0,1:T(8,128)}, u32[]{:S(2)}) copy-start(s32[32,8]{0,1:T(8,128)} %param.7) | copy-start | bytes 3076

commit v2 on v1

--- a/solution.py
+++ b/solution.py
@@ -102,9 +102,9 @@
 
 
 def fused_kernel(
-    ids_ref, logits_ref, grad_ref, rw_ref, w_hbm, saved_hbm,
-    scaled_ref, hidden_ref, input_ref,
-    w_ref, saved_ref, rows_all, probs_all, probs_own, slot_ref, slot_rows, prob_col, part,
+    ids_hbm, logits_hbm, grad_hbm, rw_hbm, w_hbm, saved_hbm,
+    wg_ref, hidden_ref, input_ref,
+    ids_ref, logits_ref, grad_ref, rw_ref, in_sem, scaled, w_ref, saved_ref, rows_all, probs_all, probs_own, slot_ref, slot_rows, prob_col, part,
     recv_a, send_b, recv_b, score_own, score_recv, score_rows,
     w_sem, saved_sem, rows_send, rows_recv, probs_send, probs_recv,
     a_send, a_recv, b_send, b_recv, sc_send, sc_recv,
@@ -135,6 +135,14 @@
                     device_id=(lax.rem(g + dg, groups), lax.rem(k + dk, parts)),
                     device_id_type=MESH,
                 )
+    small = [
+        pltpu.make_async_copy(src, dst, in_sem.at[i])
+        for i, (src, dst) in enumerate(
+            [(ids_hbm, ids_ref), (logits_hbm, logits_ref), (grad_hbm, grad_ref), (rw_hbm, rw_ref)]
+        )
+    ]
+    for copy in small:
+        copy.start()
     w_copies = [
         pltpu.make_async_copy(w_hbm.at[i], w_ref.at[i], w_sem.at[i]) for i in range(local)
     ]
@@ -143,6 +151,8 @@
     saved_copy = pltpu.make_async_copy(saved_hbm, saved_ref, saved_sem)
     saved_copy.start()
 
+    small[0].wait()
+    small[1].wait()
     sig = 1.0 / (1.0 + jnp.exp(-logits_ref[...]))
     ids = ids_ref[...]
     expert_iota = lax.broadcasted_iota(jnp.int32, (experts, rows), 0)
@@ -161,12 +171,18 @@
     ).astype(bf16)
     probs_own[...] = placed
     probs_all[g] = placed
+    small[2].wait()
     rows_all[pl.ds(pl.multiple_of(g * rows, rows), rows), :] = grad_ref[...]
 
     pl.semaphore_wait(barrier, groups * parts - 1)
 
-    parity, pos = lax.rem(g, 2), g // 2
-    mate = g + 1 - 2 * parity
+    def across(index, mask):
+        bit = 1
+        while bit <= mask:
+            if mask & bit:
+                index = index + bit - 2 * bit * lax.rem(index // bit, 2)
+            bit *= 2
+        return index
 
     def block(b):
         return rows_all.at[pl.ds(pl.multiple_of(b * rows, rows), rows), :]
@@ -178,7 +194,6 @@
         )
 
     sends = []
-    peers = [lax.rem(pos + j, half_groups) * 2 + parity for j in range(1, half_groups)]
     for j in range(1, groups):
         to = lax.rem(g + j, groups)
         copy = pltpu.make_async_remote_copy(
@@ -188,15 +203,23 @@
         )
         copy.start()
         sends.append(copy)
-    for n, to in enumerate([*peers, mate]):
-        copy = rows_copy(grad_ref, g, to, n)
-        copy.start()
-        sends.append(copy)
-    for n, peer in enumerate(peers):
-        rows_copy(block(peer), peer, g, 0).wait_recv()
-        copy = rows_copy(block(peer), peer, mate, half_groups + n)
-        copy.start()
-        sends.append(copy)
+
+    def spread(src, mask):
+        stride = groups // 2 if mask == 0 else (mask & -mask) // 2
+        while stride >= 1:
+            copy = rows_copy(src, across(g, mask), across(g, stride), mask | stride)
+            copy.start()
+            sends.append(copy)
+            stride //= 2
+
+    def arrive(mask):
+        b = across(g, mask)
+        rows_copy(block(b), b, g, 0).wait_recv()
+        spread(block(b), mask)
+
+    spread(grad_ref, 0)
+    arrive(2)
+    arrive(half_groups)
 
     for j in range(1, groups):
         b = lax.rem(g + j, groups)
@@ -240,10 +263,6 @@
             jnp.where(match, prob_tokens[l : l + 1, :], 0.0), axis=1, keepdims=True
         )
 
-    rows_copy(grad_ref, mate, g, 0).wait_recv()
-    for n, peer in enumerate(peers):
-        b = peer + 1 - 2 * parity
-        rows_copy(grad_ref, b, g, 0).wait_recv()
     for copy in w_copies:
         copy.wait()
 
@@ -265,30 +284,36 @@
 
     partner = k + 1 - 2 * core
     step = min(width, 256)
-    for l in order:
-        row = jnp.concatenate([slot_row(l, 0), slot_row(l, 1)], axis=1)
-        match = lax.broadcasted_iota(jnp.int32, (span, tokens), 0) == row
-        slot_rows[l] = jnp.dot(
-            match.astype(f32).astype(bf16), rows_all[...], preferred_element_type=f32
+    near = g // half_groups
+    far = 1 - near
+    kept = pl.ds(pl.multiple_of(core * share, share), share)
+
+    def multiply(l, half):
+        own = pl.ds(pl.multiple_of(half * share, share), share)
+        match = (
+            lax.broadcasted_iota(jnp.int32, (share, half_tokens), 0) + half * share
+            == slot_row(l, half)
+        )
+        gathered = rows_all[pl.ds(pl.multiple_of(half * half_tokens, half_tokens), half_tokens), :]
+        slot_rows[l, own, :] = jnp.dot(
+            match.astype(f32).astype(bf16), gathered, preferred_element_type=f32
         ).astype(bf16)
         for n in range(0, width, step):
-            part[l, :, n : n + step] = jnp.dot(
-                slot_rows[l], w_ref[l, :, n : n + step], preferred_element_type=f32
+            part[l, own, n : n + step] = jnp.dot(
+                slot_rows[l, own, :], w_ref[l, :, n : n + step], preferred_element_type=f32
             ).astype(bf16)
-        copy = a_copy(l, 1 - core, partner)
-        copy.start()
-        sends.append(copy)
-
-    saved_copy.wait()
-    kept = pl.ds(pl.multiple_of(core * share, share), share)
-    for i, l in enumerate(order):
+
+        @pl.when(half != core)
+        def _():
+            a_copy(l, 1 - core, partner).start()
+
+    def combine(i):
+        l = order[i]
         a_copy(l, 1 - core, partner).wait_recv()
         both = part[l, kept, :].astype(f32) + recv_a[l].astype(f32)
         send_b[l] = both.astype(bf16)
         if i < chips - 1:
-            copy = b_copy(l)
-            copy.start()
-            sends.append(copy)
+            b_copy(l).start()
         start = pl.multiple_of(l * span + core * share, share)
         score = jnp.sum(
             saved_ref[pl.ds(start, share), :].astype(f32) * both, axis=1, keepdims=True
@@ -298,6 +323,36 @@
             == slot_row(l, core)
         )
         score_own[pl.ds(l, 1), :] = jnp.sum(jnp.where(match, score, 0.0), axis=0, keepdims=True)
+
+    late = [m for m in range(half_groups + 1, groups)]
+    forwarders = [m for m in late if m % 2 == 0]
+    for mask in range(1, half_groups):
+        if mask != 2:
+            arrive(mask)
+    multiply(order[0], near)
+    for mask in forwarders:
+        arrive(mask)
+    for i in range(1, chips):
+        multiply(order[i], near)
+    saved_copy.wait()
+
+    @pl.when(near == core)
+    def _():
+        for i in range(chips - 1):
+            combine(i)
+
+    for mask in late:
+        if mask % 2:
+            arrive(mask)
+    for i in range(chips):
+        multiply(order[i], far)
+
+    @pl.when(near != core)
+    def _():
+        for i in range(chips - 1):
+            combine(i)
+
+    combine(chips - 1)
 
     def score_copy(b, to, sem, y, o):
         return pltpu.make_async_remote_copy(
@@ -322,7 +377,14 @@
         score_recv[chip, g] = score_own[...]
 
     for l in range(local):
-        scaled_ref[l] = (prob_col[l] * slot_rows[l].astype(f32)).astype(bf16)
+        scaled[l] = (prob_col[l] * slot_rows[l].astype(f32)).astype(bf16)
+        for n in range(0, features, min(features, 256)):
+            wg_ref[l, n : n + min(features, 256), :] = lax.dot_general(
+                scaled[l, :, n : n + min(features, 256)],
+                saved_ref[l * span : (l + 1) * span, :],
+                (((0,), (0,)), ((), ())),
+                preferred_element_type=f32,
+            ).astype(bf16)
 
     for i in range(chips - 1):
         source = order[i]
@@ -362,10 +424,15 @@
     turned = lax.dot_general(
         eye.astype(f32).astype(bf16), terms, (((1,), (1,)), ((), ())), preferred_element_type=f32
     ).astype(bf16)
+    small[3].wait()
     input_ref[...] = jnp.dot(turned, rw_ref[...], preferred_element_type=f32).astype(bf16)
 
     for copy in sends:
         copy.wait_send()
+    for l in order:
+        a_copy(l, 1 - core, partner).wait_send()
+    for l in order[:-1]:
+        b_copy(l).wait_send()
     for j in range(half_groups):
         b = core * half_groups + j
         for dk in range(parts):
@@ -374,6 +441,17 @@
                 wait()
             else:
                 pl.when(b != g)(wait)
+
+
+def store_kernel(a, b, c, a_out, b_out, c_out, sem):
+    copies = [
+        pltpu.make_async_copy(src, dst, sem.at[i])
+        for i, (src, dst) in enumerate([(a, a_out), (b, b_out), (c, c_out)])
+    ]
+    for copy in copies:
+        copy.start()
+    for copy in copies:
+        copy.wait()
 
 
 def fused(out_grad, expert_ids, router_logits, router_weight, expert_weight, hidden_saved):
@@ -388,18 +466,24 @@
     chips = parts // 2
     f32, bf16 = jnp.float32, jnp.bfloat16
     vmem = pl.BlockSpec(memory_space=pltpu.VMEM)
-    anyspace = pl.BlockSpec(memory_space=pl.ANY)
+    hbm = pl.BlockSpec(memory_space=pltpu.HBM)
     dma = pltpu.SemaphoreType.DMA
-    scaled, hidden, input_grad = pl.pallas_call(
+    weight_grad, hidden, input_grad = pl.pallas_call(
         fused_kernel,
         out_shape=(
-            jax.ShapeDtypeStruct((local, span, features), bf16),
+            jax.ShapeDtypeStruct((local, features, width), bf16),
             jax.ShapeDtypeStruct((share, width), bf16),
             jax.ShapeDtypeStruct((rows, features), bf16),
         ),
-        in_specs=[vmem, vmem, vmem, vmem, anyspace, anyspace],
+        in_specs=[hbm] * 6,
         out_specs=(vmem, vmem, vmem),
         scratch_shapes=[
+            pltpu.VMEM(expert_ids.shape[::-1], jnp.int32),
+            pltpu.VMEM(router_logits.shape[::-1], f32),
+            pltpu.VMEM(out_grad.shape, bf16),
+            pltpu.VMEM(router_weight.shape, bf16),
+            dma((4,)),
+            pltpu.VMEM((local, span, features), bf16),
             pltpu.VMEM((local, features, width), bf16),
             pltpu.VMEM((slots, width), bf16),
             pltpu.VMEM((groups * rows, features), bf16),
@@ -415,7 +499,7 @@
             pltpu.VMEM((local, half_tokens), f32),
             pltpu.VMEM((chips, groups, local, half_tokens), f32),
             pltpu.VMEM((experts, half_tokens), f32),
-            dma((local,)), dma, dma((groups - 1,)), dma((groups,)),
+            dma((local,)), dma, dma((groups,)), dma((groups,)),
             dma((groups - 1,)), dma((groups,)),
             dma((local,)), dma((local,)), dma((local,)), dma((chips,)),
             dma((groups // 2 * parts,)), dma((chips * groups,)),
@@ -423,14 +507,22 @@
         compiler_params=pltpu.CompilerParams(
             collective_id=0, has_side_effects=True, vmem_limit_bytes=40 * 1024 * 1024
         ),
-    )(
-        expert_ids.T, router_logits.T, out_grad, router_weight, expert_weight,
-        hidden_saved.reshape(slots, width),
-    )
-    saved_rows = hidden_saved.reshape(local, span, width)
-    weight_grad = jnp.einsum(
-        "lmd,lmf->ldf", scaled, saved_rows, preferred_element_type=f32
-    ).astype(bf16)
+    )(*[
+        pltpu.with_memory_space_constraint(x, pltpu.HBM)
+        for x in (
+            expert_ids.T, router_logits.T, out_grad, router_weight, expert_weight,
+            hidden_saved.reshape(slots, width),
+        )
+    ])
+    results = (weight_grad, hidden, input_grad)
+    weight_grad, hidden, input_grad = pl.pallas_call(
+        store_kernel,
+        out_shape=tuple(jax.ShapeDtypeStruct(r.shape, r.dtype) for r in results),
+        in_specs=[vmem] * 3,
+        out_specs=(hbm,) * 3,
+        scratch_shapes=[dma((3,))],
+        compiler_params=pltpu.CompilerParams(vmem_limit_bytes=1024 * 1024),
+    )(*results)
     return weight_grad, hidden[None], input_grad
 
 
@@ -440,7 +532,7 @@
     rows, local = out_grad.shape[0], expert_weight.shape[0]
     slots_for_one = hidden_saved.shape[1] // groups
     lanes = groups // 2 * rows
-    if parts == 2 * local and groups % 2 == 0 and rows <= slots_for_one and lanes % 128 == 0:
+    if parts == 2 * local and groups >= 4 and groups & (groups - 1) == 0 and rows <= slots_for_one and lanes % 128 == 0:
         return fused(*args)
     return body(*args)
 

time: 41.2 us -> 28.7 us (0.70)
  local copies, waits for them, and re-layouts: 7.72 us -> 0 us
  matrix products: 3.32 us -> 0 us
  Pallas kernels: 28.8 us -> 27.6 us
    unnamed x14 -> x0, local copies, waits for them, and re-layouts: 7.72 us -> none
    dot_general x1 -> x0, matrix products: 3.32 us -> none  [fused(): jnp.einsum('lmd,lmf->ldf', scaled, saved_rows, preferred_element_type=f32)]
    pallas_call x1 -> x2, Pallas kernels: 28.8 us -> 27.6 us  [the longest x1 25.4 us: fused(): pl.pallas_call(fused_kernel, out_shape=(jax.ShapeDtypeStruct((local, feat...]
where the time goes in v2:
time: 28.7 us; the launch traced here: 28.2 us
  Pallas kernels  27.6 us (96%)
  between operations  0.64 us (2%)
    pallas_call x1, Pallas kernels, fused(): pl.pallas_call(fused_kernel, out_shape=(jax.ShapeDtypeStruct((local, feat...  25.4 us
    pallas_call x1, Pallas kernels, fused(): pl.pallas_call(store_kernel, out_shape=tuple((jax.ShapeDtypeStruct(r.shap...  2.12 us

profile of v2, /device:TPU:0, one launch (start us, length us, event | category | flops | bytes accessed | tf_op | source)
XLA Modules:
  0.0 28.2 jit_solution(1313838107535788666)
XLA Ops:
  0.6 25.4 %shard_map.85 = (bf16[2,1024,1024]{2,1,0:T(8,128)(2,1)S(1)}, bf16[128,1024]{1,0:T(8,128)(2,1)S(1)}, bf16[32,1024]{1,0:T(8,128)(2,1)S(1)}) custom-call(s32[8,32]{1,0:T(8,128)} %bitcast.6, f32[16,32]{1,0:T(8,128)} %bitcast.5, bf16[32,1024]{1,0:T(8,128)(2,1)} %grad_hbm.1, bf16[16,1024]{1,0:T(8,128)(2,1)} %rw_hbm.1, bf16[2,1024,1024]{2,1,0:T(8,128)(2,1)} %w_hbm.1, ...), custom_call_target="tpu_custom_call" | custom-call | tf_op jit(solution)/shard_map/pallas_call | solution.py:471
  26.1 2.1 %shard_map.86 = (bf16[2,1024,1024]{2,1,0:T(8,128)(2,1)}, bf16[128,1024]{1,0:T(8,128)(2,1)}, bf16[32,1024]{1,0:T(8,128)(2,1)}) custom-call(bf16[2,1024,1024]{2,1,0:T(8,128)(2,1)S(1)} %get-tuple-element.9.a, bf16[128,1024]{1,0:T(8,128)(2,1)S(1)} %get-tuple-element.10.b, bf16[32,1024]{1,0:T(8,128)(2,1)S(1)} %get-tuple-element.11.c), custom_call_target="tpu_custom_call" | custom-call | tf_op jit(solution)/shard_map/pallas_call | solution.py:518

commit v3 on v2

--- a/solution.py
+++ b/solution.py
@@ -184,12 +184,20 @@
             bit *= 2
         return index
 
-    def block(b):
-        return rows_all.at[pl.ds(pl.multiple_of(b * rows, rows), rows), :]
-
-    def rows_copy(src, b, to, sem):
+    pieces = rows_recv.shape[1]
+    piece_rows = rows // pieces
+
+    def block(b, piece):
+        start = pl.multiple_of(b * rows + piece * piece_rows, piece_rows)
+        return rows_all.at[pl.ds(start, piece_rows), :]
+
+    def own_piece(piece):
+        return grad_ref.at[pl.ds(piece * piece_rows, piece_rows), :]
+
+    def rows_copy(src, b, to, sem, piece):
         return pltpu.make_async_remote_copy(
-            src_ref=src, dst_ref=block(b), send_sem=rows_send.at[sem], recv_sem=rows_recv.at[b],
+            src_ref=src, dst_ref=block(b, piece),
+            send_sem=rows_send.at[sem, piece], recv_sem=rows_recv.at[b, piece],
             device_id=(to, k), device_id_type=MESH,
         )
 
@@ -204,22 +212,24 @@
         copy.start()
         sends.append(copy)
 
-    def spread(src, mask):
+    def spread(src, mask, piece):
         stride = groups // 2 if mask == 0 else (mask & -mask) // 2
         while stride >= 1:
-            copy = rows_copy(src, across(g, mask), across(g, stride), mask | stride)
+            copy = rows_copy(src, across(g, mask), across(g, stride), mask | stride, piece)
             copy.start()
             sends.append(copy)
             stride //= 2
 
-    def arrive(mask):
+    def arrive(mask, piece):
         b = across(g, mask)
-        rows_copy(block(b), b, g, 0).wait_recv()
-        spread(block(b), mask)
-
-    spread(grad_ref, 0)
-    arrive(2)
-    arrive(half_groups)
+        rows_copy(block(b, piece), b, g, 0, piece).wait_recv()
+        spread(block(b, piece), mask, piece)
+
+    for piece in range(pieces):
+        spread(own_piece(piece), 0, piece)
+    for mask in (2, half_groups):
+        for piece in range(pieces):
+            arrive(mask, piece)
 
     for j in range(1, groups):
         b = lax.rem(g + j, groups)
@@ -327,13 +337,17 @@
     late = [m for m in range(half_groups + 1, groups)]
     forwarders = [m for m in late if m % 2 == 0]
     for mask in range(1, half_groups):
-        if mask != 2:
-            arrive(mask)
+        for piece in range(pieces):
+            if mask != 2:
+                arrive(mask, piece)
     multiply(order[0], near)
     for mask in forwarders:
-        arrive(mask)
+        arrive(mask, 0)
     for i in range(1, chips):
         multiply(order[i], near)
+    for mask in forwarders:
+        for piece in range(1, pieces):
+            arrive(mask, piece)
     saved_copy.wait()
 
     @pl.when(near == core)
@@ -342,8 +356,9 @@
             combine(i)
 
     for mask in late:
-        if mask % 2:
-            arrive(mask)
+        for piece in range(pieces):
+            if mask % 2:
+                arrive(mask, piece)
     for i in range(chips):
         multiply(order[i], far)
 
@@ -444,10 +459,20 @@
 
 
 def store_kernel(a, b, c, a_out, b_out, c_out, sem):
+    count, depth, _ = a.shape
+    cuts = (sem.shape[0] - 2) // count
+    cut = depth // cuts
     copies = [
-        pltpu.make_async_copy(src, dst, sem.at[i])
-        for i, (src, dst) in enumerate([(a, a_out), (b, b_out), (c, c_out)])
+        pltpu.make_async_copy(b, b_out, sem.at[0]), pltpu.make_async_copy(c, c_out, sem.at[1])
     ]
+    for i in range(count):
+        for j in range(cuts):
+            span = pl.ds(j * cut, cut)
+            copies.append(
+                pltpu.make_async_copy(
+                    a.at[i, span, :], a_out.at[i, span, :], sem.at[2 + i * cuts + j]
+                )
+            )
     for copy in copies:
         copy.start()
     for copy in copies:
@@ -464,6 +489,7 @@
     half_tokens = groups // 2 * rows
     share = span // 2
     chips = parts // 2
+    pieces = 2 if rows % 32 == 0 else 1
     f32, bf16 = jnp.float32, jnp.bfloat16
     vmem = pl.BlockSpec(memory_space=pltpu.VMEM)
     hbm = pl.BlockSpec(memory_space=pltpu.HBM)
@@ -499,7 +525,7 @@
             pltpu.VMEM((local, half_tokens), f32),
             pltpu.VMEM((chips, groups, local, half_tokens), f32),
             pltpu.VMEM((experts, half_tokens), f32),
-            dma((local,)), dma, dma((groups,)), dma((groups,)),
+            dma((local,)), dma, dma((groups, pieces)), dma((groups, pieces)),
             dma((groups - 1,)), dma((groups,)),
             dma((local,)), dma((local,)), dma((local,)), dma((chips,)),
             dma((groups // 2 * parts,)), dma((chips * groups,)),
@@ -520,7 +546,7 @@
         out_shape=tuple(jax.ShapeDtypeStruct(r.shape, r.dtype) for r in results),
         in_specs=[vmem] * 3,
         out_specs=(hbm,) * 3,
-        scratch_shapes=[dma((3,))],
+        scratch_shapes=[dma((2 + 4 * local,))],
         compiler_params=pltpu.CompilerParams(vmem_limit_bytes=1024 * 1024),
     )(*results)
     return weight_grad, hidden[None], input_grad

time: 28.7 us -> 29.2 us (1.017)
  the two profiles are of different devices: /device:TPU:0 before, /device:TPU:1 now
where the time goes in v3:
time: 29.2 us; the launch traced here: 29.1 us
  Pallas kernels  28.4 us (97%)
  between operations  0.64 us (2%)
    pallas_call x1, Pallas kernels, fused(): pl.pallas_call(fused_kernel, out_shape=(jax.ShapeDtypeStruct((local, feat...  26.2 us
    pallas_call x1, Pallas kernels, fused(): pl.pallas_call(store_kernel, out_shape=tuple((jax.ShapeDtypeStruct(r.shap...  2.2 us

profile of v3, /device:TPU:1, one launch (start us, length us, event | category | flops | bytes accessed | tf_op | source)
XLA Modules:
  0.0 29.1 jit_solution(13074251008009604268)
XLA Ops:
  0.6 26.2 %shard_map.85 = (bf16[2,1024,1024]{2,1,0:T(8,128)(2,1)S(1)}, bf16[128,1024]{1,0:T(8,128)(2,1)S(1)}, bf16[32,1024]{1,0:T(8,128)(2,1)S(1)}) custom-call(s32[8,32]{1,0:T(8,128)} %bitcast.6, f32[16,32]{1,0:T(8,128)} %bitcast.5, bf16[32,1024]{1,0:T(8,128)(2,1)} %grad_hbm.1, bf16[16,1024]{1,0:T(8,128)(2,1)} %rw_hbm.1, bf16[2,1024,1024]{2,1,0:T(8,128)(2,1)} %w_hbm.1, ...), custom_call_target="tpu_custom_call" | custom-call | tf_op jit(solution)/shard_map/pallas_call | solution.py:497
  26.9 2.2 %shard_map.86 = (bf16[2,1024,1024]{2,1,0:T(8,128)(2,1)}, bf16[128,1024]{1,0:T(8,128)(2,1)}, bf16[32,1024]{1,0:T(8,128)(2,1)}) custom-call(bf16[2,1024,1024]{2,1,0:T(8,128)(2,1)S(1)} %get-tuple-element.9.a, bf16[128,1024]{1,0:T(8,128)(2,1)S(1)} %get-tuple-element.10.b, bf16[32,1024]{1,0:T(8,128)(2,1)S(1)} %get-tuple-element.11.c), custom_call_target="tpu_custom_call" | custom-call | tf_op jit(solution)/shard_map/pallas_call | solution.py:544
